TPU v7x, 16 devices: a 4x2x1 block of a 4x4x4 slice. The times are simulated.
16 devices in a mesh: dp: 4 (over y, z, core), tp: 4 (over x).
Axes of the slice: x: 4, y: 2, z: 1, core: 2. Of those that a mesh axis runs over, the one named last changes fastest.
The devices are a block of a 4x4x4 slice.
Arguments:
- x: bfloat16 [256, 3072], P('dp'), parts along dimension 0
- k_cache: bfloat16 [256, 1024, 32, 96], P('dp', None, 'tp'), parts along dimension 0
- v_cache: bfloat16 [256, 1024, 32, 96], P('dp', None, 'tp'), parts along dimension 0
- gain_a: bfloat16 [3072], replicated
- wq: bfloat16 [3072, 3072], P(None, 'tp')
- wo: bfloat16 [3072, 3072], P('tp')
- gain_m: bfloat16 [3072], replicated
- w_gate: bfloat16 [3072, 8192], P(None, 'tp')
- w_up: bfloat16 [3072, 8192], P(None, 'tp')
- w_down: bfloat16 [8192, 3072], P('tp')
Outputs:
- output: bfloat16 [256, 3072], P('dp'), parts along dimension 0
There are 4 independent parts. A program takes and returns all parts, laid end to end along the dimension named above; an argument that names none is the same for every part.
All inputs are finite; a program needn't handle non-finite values.
Results may differ from a plain program's by a relative error of at most 0.017.
Values are sent between devices in bfloat16 or wider.
A program may use at most 1.5 GiB of HBM per device.

v0:
```python
import jax
import jax.numpy as jnp
from jax import lax
from jax.sharding import PartitionSpec as P

HEAD = 96
THETA = 10000


def normed(x, gain):
    wide = x.astype(jnp.float32)
    scale = lax.rsqrt(jnp.mean(wide * wide, -1, keepdims=True) + 1e-6)
    return (wide * scale * gain.astype(jnp.float32)).astype(jnp.bfloat16)


def turned(t, place, theta):
    half = t.shape[-1] // 2
    angle = place.astype(jnp.float32)[:, None] * theta ** (-jnp.arange(half, dtype=jnp.float32) / half)
    cos, sin = jnp.cos(angle)[:, None], jnp.sin(angle)[:, None]
    a, b = t[..., :half].astype(jnp.float32), t[..., half:].astype(jnp.float32)
    return jnp.concatenate([a * cos - b * sin, b * cos + a * sin], -1).astype(jnp.bfloat16)


def matmul(a, w):
    return jnp.dot(a, w, preferred_element_type=jnp.float32).astype(jnp.bfloat16)


def einsum(form, a, b):
    return jnp.einsum(form, a.astype(jnp.float32), b.astype(jnp.float32))


def seen_by(a, wq, k_cache, v_cache, head, theta):
    batch, cache, kv_heads = k_cache.shape[:3]
    place = jnp.full((batch,), cache - 1)
    q = turned(matmul(a, wq).reshape(batch, -1, head), place, theta).reshape(batch, kv_heads, -1, head)
    scores = einsum("bgsd,bugd->bgsu", q, k_cache) * head**-0.5
    weights = jax.nn.softmax(scores, -1).astype(jnp.bfloat16)
    return einsum("bgsu,bugd->bgsd", weights, v_cache).astype(jnp.bfloat16).reshape(batch, -1)


def hidden_of(b, w_gate, w_up):
    gate = jnp.dot(b, w_gate, preferred_element_type=jnp.float32)
    up = jnp.dot(b, w_up, preferred_element_type=jnp.float32)
    return (jax.nn.silu(gate) * up).astype(jnp.bfloat16)


def solution(mesh):
    def added(t, term):
        return (t.astype(jnp.float32) + lax.psum(term.astype(jnp.bfloat16), "tp").astype(jnp.float32)).astype(jnp.bfloat16)

    def step(x, k_cache, v_cache, gain_a, wq, wo, gain_m, w_gate, w_up, w_down):
        seen = seen_by(normed(x, gain_a), wq, k_cache, v_cache, HEAD, THETA)
        h = added(x, jnp.dot(seen, wo, preferred_element_type=jnp.float32))
        return added(h, jnp.dot(hidden_of(normed(h, gain_m), w_gate, w_up), w_down, preferred_element_type=jnp.float32))

    states, cache, columns, rows_of = P("dp", None), P("dp", None, "tp", None), P(None, "tp"), P("tp", None)
    return jax.shard_map(
        step,
        mesh=mesh,
        in_specs=(states, cache, cache, P(None), columns, rows_of, P(None), columns, columns, rows_of),
        out_specs=states,
        check_vma=False,
    )
```

profile of v0, /device:TPU:112, one launch (start us, length us, event | category | flops | bytes accessed | tf_op | source)
XLA Modules:
  0.0 189.4 jit_solution(15106165594503827404)
XLA Ops:
  6.5 0.0 all-reduce.3.cloned.1.call-start
  6.6 0.7 convert_element_type.66
  7.3 1.2 fusion.8
  8.5 3.5 %convolution_convert_fusion.2 = bf16[64,768]{1,0:T(8,128)(2,1)S(1)} fusion(bf16[3072,768]{1,0:T(8,128)(2,1)} %param.14, bf16[64,3072]{1,0:T(8,128)(2,1)} %param.10, f32[3072]{0:T(1024)S(1)} %convert_element_type.66, f32[64]{0:T(128)S(1)} %add_rsqrt_fusion.1), kind=kOutput, calls=%fused_computation.19 | convolution fusion | flops 302825472 | bytes 5222656 | tf_op jit(solution)/shard_map/dot_general | solution.py:25
  12.0 0.2 reshape.61
  12.1 0.1 fusion.25
  12.3 0.1 maximum_bitcast_fusion
  12.4 33.3 %fusion.28 = f32[64,8,1,1024]{3,2,1,0:T(1,128)S(1)} fusion(bf16[64,1024,8,96]{1,3,2,0:T(8,128)(2,1)} %param.11, bf16[64,8,96,1]{2,1,0,3:T(8,128)(2,1)S(1)} %maximum_bitcast_fusion), kind=kOutput, calls=%fused_computation.44 | convolution fusion | flops 100663296 | bytes 102858752 | tf_op jit(solution)/shard_map/bgsd,bugd->bgsu/dot_general | solution.py:29
  45.7 1.1 fusion.6
  46.8 36.4 %fusion.3 = f32[64,8,1,96]{3,2,1,0:T(1,128)S(1)} fusion(bf16[64,1024,8,96]{1,3,2,0:T(8,128)(2,1)} %param.12, bf16[64,8,1024,1]{2,1,0,3:T(8,128)(2,1)S(1)} %fusion.6), kind=kOutput, calls=%fused_computation.7 | convolution fusion | flops 100663296 | bytes 101908480 | tf_op jit(solution)/shard_map/bgsu,bugd->bgsd/dot_general | solution.py:29
  83.2 0.0 copy-start.1
  83.2 0.0 copy-start
  83.2 0.1 reshape.62
  83.4 4.0 %convolution_convert_fusion = bf16[64,3072]{1,0:T(8,128)(2,1)} fusion(bf16[64,768]{1,0:T(8,128)(2,1)S(1)} %reshape.62, bf16[768,3072]{1,0:T(8,128)(2,1)} %param.15), kind=kOutput, calls=%fused_computation.2 | convolution fusion | flops 302186496 | bytes 5210112 | tf_op jit(solution)/shard_map/dot_general | solution.py:53
  87.4 0.1 all-reduce.3.cloned.1.call-update
  87.5 0.2 all-reduce.5.cloned.1.call-start
  87.7 0.0 copy-done.1
  87.7 36.7 %all-reduce.3.cloned.1.call-done = bf16[64,3072]{1,0:T(8,128)(2,1)} async-done(((bf16[64,3072]{1,0:T(8,128)(2,1)}), bf16[64,3072]{1,0:T(8,128)(2,1)}) %all-reduce.3.cloned.1.call-update) | async-done | bytes 393232 | tf_op jit(solution)/shard_map/psum | solution.py:49
  124.4 0.0 copy-done
  124.4 1.2 fusion.12
  125.7 6.9 %fusion.33 = f32[64,2048]{1,0:T(8,128)S(1)} fusion(bf16[3072,2048]{1,0:T(8,128)(2,1)} %param.17, bf16[64,3072]{1,0:T(8,128)(2,1)S(1)} %get-tuple-element.6, f32[3072]{0:T(1024)S(1)} %convert_element_type.77, f32[64]{0:T(128)S(1)} %add_rsqrt_fusion), kind=kOutput, calls=%fused_computation.48 | convolution fusion | flops 806092800 | bytes 13512960 | tf_op jit(solution)/shard_map/dot_general | solution.py:42
  132.6 13.4 %convolution_convert_fusion.1 = bf16[64,3072]{1,0:T(8,128)(2,1)} fusion(bf16[2048,3072]{1,0:T(8,128)(2,1)} %param.19, bf16[3072,2048]{1,0:T(8,128)(2,1)} %param.18, f32[64,2048]{1,0:T(8,128)S(1)} %fusion.33, bf16[64,3072]{1,0:T(8,128)(2,1)S(1)} %get-tuple-element.6, f32[3072]{0:T(1024)S(1)} %convert_element_type.77, f32[64]{0:T(128)S(1)} %add_rsqrt_fusion), kind=kOutput, calls=%fused_computation.3 | convolution fusion | flops 1612382208 | bytes 26489088 | tf_op jit(solution)/shard_map/dot_general | solution.py:54
  146.1 0.1 all-reduce.5.cloned.1.call-update
  146.1 34.6 %all-reduce.5.cloned.1.call-done = bf16[64,3072]{1,0:T(8,128)(2,1)} async-done(((bf16[64,3072]{1,0:T(8,128)(2,1)}), bf16[64,3072]{1,0:T(8,128)(2,1)}) %all-reduce.5.cloned.1.call-update) | async-done | bytes 393232 | tf_op jit(solution)/shard_map/psum | solution.py:49
  180.7 1.8 fusion.15
  (5 shorter events, 0.1 us)
Async XLA Ops:
  6.5 117.9 %all-reduce.3.cloned.1.call-start = ((), (), s32[]{:S(2)}) async-start(), calls=%async_computation | async-start | bytes 786432 | tf_op jit(solution)/shard_map/psum | solution.py:49
  83.2 4.5 %copy-start.1 = (bf16[3072]{0:T(1024)(128)(2,1)S(1)}, bf16[3072]{0:T(1024)(128)(2,1)}, u32[]{:S(2)}) copy-start(bf16[3072]{0:T(1024)(128)(2,1)} %param.16) | copy-start | bytes 18436
  83.2 41.2 %copy-start = (bf16[64,3072]{1,0:T(8,128)(2,1)S(1)}, bf16[64,3072]{1,0:T(8,128)(2,1)}, u32[]{:S(2)}) copy-start(bf16[64,3072]{1,0:T(8,128)(2,1)} %param.10) | copy-start | bytes 1179652
  87.5 93.3 %all-reduce.5.cloned.1.call-start = ((), (), s32[]{:S(2)}) async-start(), calls=%async_computation.1 | async-start | bytes 786432 | tf_op jit(solution)/shard_map/psum | solution.py:49
Sparse Core Ops, SparseCore 0:
  87.6 36.7 all-reduce.2
  146.2 34.4 all-reduce.4
where the time goes:
time: 190 us; the launch traced here: 189 us
  matrix products  97.5 us (51%)
  waiting for transfers between devices  71.4 us (38%)
  between operations  13.5 us (7%)
  other arithmetic  6.4 us (3%)
    psum x2, waiting for transfers between devices, added(): lax.psum(term.astype(jnp.bfloat16), 'tp').astype(jnp.float32)  71.3 us
    dot_general x2, matrix products, einsum(): return jnp.einsum(form, a.astype(jnp.float32), b.astype(jnp.float32))  69.7 us
    dot_general x1, matrix products, step(): jnp.dot(hidden_of(normed(h, gain_m), w_gate, w_up), w_down, preferred_ele...  13.4 us
    dot_general x1, matrix products, hidden_of(): gate = jnp.dot(b, w_gate, preferred_element_type=jnp.float32)  6.94 us
    dot_general x1, matrix products, step(): h = added(x, jnp.dot(seen, wo, preferred_element_type=jnp.float32))  4.02 us
  transfers between devices with their start and end apart: 2, of which 2 were waited for; matrix products, arithmetic and copies ran while one was open for 0% of the time, Pallas kernels for 0%

commit v1 on v0

v1 whole, which is shorter than its diff:
```python
import functools

import jax
import jax.numpy as jnp
import numpy as np
from jax import lax
from jax.experimental import pallas as pl
from jax.experimental.pallas import tpu as pltpu
from jax.sharding import PartitionSpec as P

HEAD = 96
THETA = 10000
MESH = pl.DeviceIdType.MESH
F32, BF16 = jnp.float32, jnp.bfloat16
PAIR = 2
RING = 3
COLS = 512
EARLY = 48
VMEM_BYTES = 67_043_328


def dot(a, b):
    return lax.dot_general(a, b, (((1,), (0,)), ((), ())), preferred_element_type=F32)


def dot_t(a, b):
    return lax.dot_general(a, b, (((1,), (1,)), ((), ())), preferred_element_type=F32)


def kernel(n, x_hbm, k_hbm, v_hbm, ga_hbm, gm_hbm, turn_hbm, wq_hbm, wo_hbm, wg_hbm, wu_hbm, wd_hbm, out,
           xv, gav, gmv, turnv, gv, uv, dv, wov, kbuf, vbuf, q_s, s_s, seen, normed, hbuf, hidden,
           acc, t1, rs1, t2, rs2, ybuf,
           sem_in, sem_k, sem_v, sem_w, sem_d, send1, recv1, gsend1, grecv1, send2, recv2, gsend2, grecv2):
    batch, d = xv.shape
    width = d // n
    inner = q_s.shape[1]
    heads = inner // HEAD
    rows = PAIR * heads
    steps = batch // PAIR
    chunks = gv.shape[0]
    me = lax.axis_index("tp")

    def peer(j):
        return lax.rem(me + j, n)

    def block_of(j):
        return pl.ds(pl.multiple_of(peer(j) * width, width), width)

    copy = pltpu.make_async_copy
    x_in = copy(x_hbm, xv, sem_in.at[0])
    ga_in = copy(ga_hbm, gav, sem_in.at[1])
    gm_in = copy(gm_hbm, gmv, sem_in.at[2])
    turn_in = copy(turn_hbm, turnv, sem_in.at[3])
    wq_ins = []
    for c in range(0, inner, COLS):
        size = min(COLS, inner - c)
        wq_ins.append((c, size, copy(wq_hbm.at[:, pl.ds(c, size)], gv.at[c // COLS, :, pl.ds(0, size)], sem_w.at[0, c // COLS])))
    wo_in = copy(wo_hbm, wov, sem_in.at[4])

    def k_in(p):
        slot = lax.rem(p, RING)
        return copy(k_hbm.at[pl.ds(p * PAIR, PAIR)], kbuf.at[slot], sem_k.at[slot])

    def v_in(p):
        slot = lax.rem(p, RING)
        return copy(v_hbm.at[pl.ds(p * PAIR, PAIR)], vbuf.at[slot], sem_v.at[slot])

    def gate_in(c):
        return copy(wg_hbm.at[:, pl.ds(pl.multiple_of(c * COLS, COLS), COLS)], gv.at[c], sem_w.at[0, c])

    def up_in(c):
        return copy(wu_hbm.at[:, pl.ds(pl.multiple_of(c * COLS, COLS), COLS)], uv.at[c], sem_w.at[1, c])

    def down_in(j):
        return copy(wd_hbm.at[:, block_of(j)], dv.at[j], sem_d.at[j])

    x_in.start()
    ga_in.start()
    turn_in.start()
    for _, _, c in wq_ins:
        c.start()
    gm_in.start()
    for p in range(RING):
        k_in(p).start()
        v_in(p).start()
    wo_in.start()

    barrier = pltpu.get_barrier_semaphore()
    for j in range(1, n):
        pl.semaphore_signal(barrier, inc=1, device_id={"tp": peer(j)}, device_id_type=MESH)
    pl.semaphore_wait(barrier, n - 1)

    def norm_rows(parts, gain, r, many):
        wide = [part(r, many).astype(F32) for part in parts]
        total = sum(jnp.sum(w * w, -1, keepdims=True) for w in wide)
        scale = lax.rsqrt(total / d + 1e-6)
        step = d // len(parts)
        for i, w in enumerate(wide):
            at = pl.ds(i * step, step)
            normed[pl.ds(r, many), at] = (w * scale * gain[:, at].astype(F32)).astype(BF16)

    x_in.wait()
    ga_in.wait()
    for r in range(0, batch, 16):
        norm_rows([lambda r, many: xv[pl.ds(r, many), :]], gav, r, 16)
    turn_in.wait()
    for c, size, c_in in wq_ins:
        c_in.wait()
        q_s[:, pl.ds(c, size)] = dot(normed[...], gv[c // COLS, :, pl.ds(0, size)])
    half = HEAD // 2
    lane = lax.broadcasted_iota(jnp.int32, (16, inner), 1)
    first = lax.rem(lane, HEAD) < half
    for r in range(0, batch, 16):
        q = q_s[pl.ds(r, 16), :].astype(BF16).astype(F32)
        other = jnp.where(first, pltpu.roll(q, inner - half, 1), pltpu.roll(q, half, 1))
        q_s[pl.ds(r, 16), :] = q * turnv[pl.ds(0, 1), :] + other * turnv[pl.ds(1, 1), :]

    row = lax.broadcasted_iota(jnp.int32, (rows, inner), 0)
    mine = lax.broadcasted_iota(jnp.int32, (rows, inner), 1) // HEAD == lax.rem(row, heads)

    def scores(p):
        slot = lax.rem(p, RING)
        q = jnp.concatenate(
            [jnp.broadcast_to(q_s[pl.ds(p * PAIR + i, 1), :], (heads, inner)) for i in range(PAIR)], 0
        )
        q = jnp.where(mine, q, 0.0).astype(BF16)
        for i in range(PAIR):
            at = pl.ds(i * heads, heads)
            s_s[at, :] = dot(q, kbuf[slot, i])[i * heads : (i + 1) * heads]

    def attend(p, last):
        v_in(p).wait()
        if not last:
            k_in(p + 1).wait()
        s = s_s[...] * HEAD**-0.5
        e = jnp.exp(s - jnp.max(s, -1, keepdims=True))
        w = (e * (1.0 / jnp.sum(e, -1, keepdims=True))).astype(BF16)
        if not last:
            scores(p + 1)
        slot = lax.rem(p, RING)
        for i in range(PAIR):
            o = dot_t(w, vbuf[slot, i])[i * heads : (i + 1) * heads]
            seen[pl.ds(p * PAIR + i, 1), :] = jnp.sum(
                jnp.where(mine[i * heads : (i + 1) * heads], o, 0.0), 0, keepdims=True
            )

        if not last:
            @pl.when(p + 1 + RING < steps)
            def _():
                k_in(p + 1 + RING).start()

            @pl.when(p + RING < steps)
            def _():
                v_in(p + RING).start()

    order = [2, 1, 3] if n == 4 else list(range(1, n))

    def terms_out(part, r, many):
        at = pl.ds(r, many)
        a = seen[at, :].astype(BF16)
        sent = []
        for j in order:
            t1[j - 1, at, :] = dot(a, wov[:, block_of(j)]).astype(BF16)
            c = pltpu.make_async_remote_copy(
                t1.at[j - 1, at], rs1.at[j - 1, at], send1.at[part, j - 1], recv1.at[part, j - 1],
                device_id={"tp": peer(j)}, device_id_type=MESH,
            )
            c.start()
            sent.append(c)
        acc[at, :] = dot(a, wov[:, block_of(0)])
        return sent

    def states_out(part, r, many, arrived):
        at = pl.ds(r, many)
        for c in arrived:
            c.wait_recv()
        total = acc[at, :]
        for j in range(1, n):
            total = total + rs1[j - 1, at, :].astype(F32)
        hbuf[me, at, :] = (xv[at, block_of(0)].astype(F32) + total).astype(BF16)
        sent = []
        for j in order:
            c = pltpu.make_async_remote_copy(
                hbuf.at[me, at], hbuf.at[me, at], gsend1.at[part, j - 1], grecv1.at[part, j - 1],
                device_id={"tp": peer(j)}, device_id_type=MESH,
            )
            c.start()
            sent.append(c)
        return sent

    def attend_all(lo, hi):
        def body(p, carry):
            attend(p, False)
            return carry

        lax.fori_loop(lo, hi, body, 0)

    k_in(0).wait()
    scores(0)
    k_in(RING).start()
    early_steps = EARLY // PAIR
    between = early_steps + (steps - early_steps) // 2
    attend_all(0, early_steps)
    wo_in.wait()
    out_a = terms_out(0, 0, EARLY)
    attend_all(early_steps, between)
    all_a = states_out(0, 0, EARLY, out_a)
    attend_all(between, steps - RING)
    for c in range(chunks):
        gate_in(c).start()
        up_in(c).start()
    for j in order + [0]:
        down_in(j).start()
    attend_all(steps - RING, steps - 1)
    attend(steps - 1, True)
    out_b = terms_out(1, EARLY, batch - EARLY)
    all_b = states_out(1, EARLY, batch - EARLY, out_b)
    for c in all_a + all_b:
        c.wait_recv()

    gm_in.wait()
    for r in range(0, batch, 16):
        norm_rows([lambda r, many, i=i: hbuf[i, pl.ds(r, many), :] for i in range(n)], gmv, r, 16)

    def hidden_step(c, carry):
        gate_in(c).wait()
        up_in(c).wait()
        g = dot(normed[...], gv[c])
        u = dot(normed[...], uv[c])
        hidden[:, pl.ds(pl.multiple_of(c * COLS, COLS), COLS)] = (jax.nn.silu(g) * u).astype(BF16)
        return carry

    lax.fori_loop(0, chunks, hidden_step, 0)
    sent2 = []
    for j in order:
        down_in(j).wait()
        t2[j - 1] = dot(hidden[...], dv[j]).astype(BF16)
        c = pltpu.make_async_remote_copy(
            t2.at[j - 1], rs2.at[j - 1], send2.at[j - 1], recv2.at[j - 1],
            device_id={"tp": peer(j)}, device_id_type=MESH,
        )
        c.start()
        sent2.append(c)
    down_in(0).wait()
    total = dot(hidden[...], dv[0])
    acc[...] = total
    for c in sent2:
        c.wait_recv()
    total = acc[...]
    for j in range(1, n):
        total = total + rs2[j - 1].astype(F32)
    ybuf[me] = (hbuf[me].astype(F32) + total).astype(BF16)
    all_y = []
    for j in order:
        c = pltpu.make_async_remote_copy(
            ybuf.at[me], ybuf.at[me], gsend2.at[j - 1], grecv2.at[j - 1],
            device_id={"tp": peer(j)}, device_id_type=MESH,
        )
        c.start()
        all_y.append(c)
    for c in all_y:
        c.wait_recv()
    for i in range(n):
        out[:, pl.ds(i * width, width)] = ybuf[i]
    for c in out_a + out_b + all_a + all_b + sent2 + all_y:
        c.wait_send()


def turns(place, inner):
    half = HEAD // 2
    angle = np.float32(place) * np.float32(THETA) ** (-np.arange(half, dtype=np.float32) / np.float32(half))
    cos, sin = np.cos(angle.astype(np.float32)), np.sin(angle.astype(np.float32))
    one = np.stack([np.concatenate([cos, cos]), np.concatenate([-sin, sin])])
    return np.tile(one, (1, inner // HEAD)).astype(np.float32)


def solution(mesh):
    n = mesh.shape["tp"]

    def step(x, k_cache, v_cache, gain_a, wq, wo, gain_m, w_gate, w_up, w_down):
        batch, d = x.shape
        places, heads, head = k_cache.shape[1:]
        inner, ff = heads * head, w_gate.shape[1]
        width = d // n
        turn = jnp.asarray(turns(places - 1, inner))

        def rows_first(c):
            return jnp.transpose(c, (0, 2, 3, 1)).reshape(batch, inner, places)

        anywhere = pl.BlockSpec(memory_space=pl.ANY)
        dma = pltpu.SemaphoreType.DMA
        moved = n - 1
        return pl.pallas_call(
            functools.partial(kernel, n),
            name="layer",
            out_shape=jax.ShapeDtypeStruct((batch, d), BF16),
            in_specs=[anywhere] * 11,
            out_specs=pl.BlockSpec(memory_space=pltpu.VMEM),
            scratch_shapes=[
                pltpu.VMEM((batch, d), BF16),
                pltpu.VMEM((1, d), BF16),
                pltpu.VMEM((1, d), BF16),
                pltpu.VMEM((2, inner), F32),
                pltpu.VMEM((ff // COLS, d, COLS), BF16),
                pltpu.VMEM((ff // COLS, d, COLS), BF16),
                pltpu.VMEM((n, ff, width), BF16),
                pltpu.VMEM((inner, d), BF16),
                pltpu.VMEM((RING, PAIR, inner, places), BF16),
                pltpu.VMEM((RING, PAIR, inner, places), BF16),
                pltpu.VMEM((batch, inner), F32),
                pltpu.VMEM((PAIR * heads, places), F32),
                pltpu.VMEM((batch, inner), F32),
                pltpu.VMEM((batch, d), BF16),
                pltpu.VMEM((n, batch, width), BF16),
                pltpu.VMEM((batch, ff), BF16),
                pltpu.VMEM((batch, width), F32),
                pltpu.VMEM((moved, batch, width), BF16),
                pltpu.VMEM((moved, batch, width), BF16),
                pltpu.VMEM((moved, batch, width), BF16),
                pltpu.VMEM((moved, batch, width), BF16),
                pltpu.VMEM((n, batch, width), BF16),
                dma((5,)),
                dma((RING,)),
                dma((RING,)),
                dma((2, ff // COLS)),
                dma((n,)),
            ]
            + [dma((2, moved))] * 4
            + [dma((moved,))] * 4,
            compiler_params=pltpu.CompilerParams(
                collective_id=0, has_side_effects=True, vmem_limit_bytes=VMEM_BYTES
            ),
        )(
            x, rows_first(k_cache), rows_first(v_cache), gain_a.reshape(1, d), gain_m.reshape(1, d), turn,
            wq, wo, w_gate, w_up, w_down,
        )

    states, cache, columns, rows_of = P("dp", None), P("dp", None, "tp", None), P(None, "tp"), P("tp", None)
    return jax.shard_map(
        step,
        mesh=mesh,
        in_specs=(states, cache, cache, P(None), columns, rows_of, P(None), columns, columns, rows_of),
        out_specs=states,
        check_vma=False,
    )
```

time: 190 us -> 108 us (0.57)
  Pallas kernels: 0 us -> 104 us
  matrix products: 97.5 us -> 0 us
  waiting for transfers between devices: 71.4 us -> 0 us
  between operations: 13.5 us -> 0.01 us
  other arithmetic: 6.4 us -> 0 us
  local copies, waits for them, and re-layouts: 0.3 us -> 4.36 us
    pallas_call x0 -> x1, Pallas kernels: none -> 104 us  [step(): pl.pallas_call(functools.partial(kernel, n), name='layer', out_shape=jax....]
    dot_general x6 -> x0, matrix products: 97.5 us -> none  [the longest x2 69.7 us: einsum(): return jnp.einsum(form, a.astype(jnp.float32), b.astype(jnp.float32))]
    psum x2 -> x0, waiting for transfers between devices: 71.3 us -> none  [added(): lax.psum(term.astype(jnp.bfloat16), 'tp').astype(jnp.float32)]
    convert_element_type x4 -> x0, other arithmetic: 2.55 us -> none  [the longest x1 1.83 us: added(): (t.astype(jnp.float32) + lax.psum(term.astype(jnp.bfloat16), 'tp').astype...]
    reduce_sum x2 -> x0, other arithmetic: 2.41 us -> none  [normed(): scale = lax.rsqrt(jnp.mean(wide * wide, -1, keepdims=True) + 1e-06)]
    reshape x2, local copies, waits for them, and re-layouts: 0.29 us -> 2.59 us  [the longest x1 1.3 us: step(): gain_a.reshape(1, d)]
  transfers between devices with their start and end apart: 2 -> 0, of which waited for: 2 -> 0; matrix products, arithmetic and copies ran while one was open for 0% -> 0% of each run, Pallas kernels for 0% -> 0%
where the time goes in v1:
time: 108 us
  Pallas kernels  104 us (96%)
  local copies, waits for them, and re-layouts  4.36 us (4%)
    pallas_call x1, Pallas kernels, step(): pl.pallas_call(functools.partial(kernel, n), name='layer', out_shape=jax....  104 us

profile of v1, /device:TPU:112, one launch (start us, length us, event | category | flops | bytes accessed | tf_op | source)
XLA Modules:
  0.0 107.9 jit_solution(2196416230366451299)
XLA Ops:
  0.0 1.3 %reshape.14.ga_hbm = bf16[1,3072]{1,0:T(2,128)(2,1)} reshape(bf16[3072]{0:T(1024)(128)(2,1)} %param.14) | data formatting | bytes 12288 | tf_op jit(solution)/shard_map/reshape | solution.py:334
  1.3 1.3 %reshape.15.gm_hbm = bf16[1,3072]{1,0:T(2,128)(2,1)} reshape(bf16[3072]{0:T(1024)(128)(2,1)} %param.17) | data formatting | bytes 12288 | tf_op jit(solution)/shard_map/reshape | solution.py:334
  2.6 103.5 %layer.1 = bf16[64,3072]{1,0:T(8,128)(2,1)} custom-call(bf16[64,3072]{1,0:T(8,128)(2,1)} %x_hbm.1, bf16[64,768,1024]{2,1,0:T(8,128)(2,1)} %bitcast.1.k_hbm, bf16[64,768,1024]{2,1,0:T(8,128)(2,1)} %bitcast.3.v_hbm, bf16[1,3072]{1,0:T(2,128)(2,1)} %reshape.14.ga_hbm, bf16[1,3072]{1,0:T(2,128)(2,1)} %reshape.15.gm_hbm, f32[2,768]{1,0:T(2,128)} %constant.2.clone.turn_hbm, ...), custom_call_target="tpu_custom_call" | custom-call | tf_op jit(solution)/shard_map/layer/pallas_call | solution.py:293
  106.1 1.8 %copy.13 = bf16[64,3072]{1,0:T(8,128)(2,1)} copy(bf16[64,3072]{1,0:T(8,128)(2,1)} %layer.1) | data formatting | bytes 786432

commit v2 on v1

--- a/solution.py
+++ b/solution.py
@@ -16,7 +16,7 @@
 RING = 3
 COLS = 512
 EARLY = 48
-VMEM_BYTES = 67_043_328
+VMEM_BYTES = 66_400_000
 
 
 def dot(a, b):
@@ -28,7 +28,7 @@
 
 
 def kernel(n, x_hbm, k_hbm, v_hbm, ga_hbm, gm_hbm, turn_hbm, wq_hbm, wo_hbm, wg_hbm, wu_hbm, wd_hbm, out,
-           xv, gav, gmv, turnv, gv, uv, dv, wov, kbuf, vbuf, q_s, s_s, seen, normed, hbuf, hidden,
+           xv, gav, gmv, gaf, gmf, turnv, gv, uv, dv, wov, kbuf, vbuf, q_s, s_s, seen, normed, hbuf, hidden,
            acc, t1, rs1, t2, rs2, ybuf,
            sem_in, sem_k, sem_v, sem_w, sem_d, send1, recv1, gsend1, grecv1, send2, recv2, gsend2, grecv2):
     batch, d = xv.shape
@@ -85,10 +85,15 @@
         v_in(p).start()
     wo_in.start()
 
-    barrier = pltpu.get_barrier_semaphore()
-    for j in range(1, n):
-        pl.semaphore_signal(barrier, inc=1, device_id={"tp": peer(j)}, device_id_type=MESH)
-    pl.semaphore_wait(barrier, n - 1)
+    with jax.named_scope("entry"):
+        barrier = pltpu.get_barrier_semaphore()
+        for j in range(1, n):
+            pl.semaphore_signal(barrier, inc=1, device_id={"tp": peer(j)}, device_id_type=MESH)
+        pl.semaphore_wait(barrier, n - 1)
+
+    def widened(gain):
+        g = gain[...].astype(F32)
+        return jnp.concatenate([g[i : i + 1] for i in range(d // 128)], 1)
 
     def norm_rows(parts, gain, r, many):
         wide = [part(r, many).astype(F32) for part in parts]
@@ -97,15 +102,18 @@
         step = d // len(parts)
         for i, w in enumerate(wide):
             at = pl.ds(i * step, step)
-            normed[pl.ds(r, many), at] = (w * scale * gain[:, at].astype(F32)).astype(BF16)
-
-    x_in.wait()
-    ga_in.wait()
+            normed[pl.ds(r, many), at] = (w * scale * gain[:, at]).astype(BF16)
+
+    with jax.named_scope("x_wait"):
+        x_in.wait()
+        ga_in.wait()
+    gaf[...] = widened(gav)
     for r in range(0, batch, 16):
-        norm_rows([lambda r, many: xv[pl.ds(r, many), :]], gav, r, 16)
+        norm_rows([lambda r, many: xv[pl.ds(r, many), :]], gaf, r, 16)
     turn_in.wait()
     for c, size, c_in in wq_ins:
-        c_in.wait()
+        with jax.named_scope("wq_wait"):
+            c_in.wait()
         q_s[:, pl.ds(c, size)] = dot(normed[...], gv[c // COLS, :, pl.ds(0, size)])
     half = HEAD // 2
     lane = lax.broadcasted_iota(jnp.int32, (16, inner), 1)
@@ -154,116 +162,167 @@
                 v_in(p + RING).start()
 
     order = [2, 1, 3] if n == 4 else list(range(1, n))
-
-    def terms_out(part, r, many):
-        at = pl.ds(r, many)
+    places = order + [0]
+    by_two = [places[i : i + 2] for i in range(0, n, 2)]
+    parts = [(0, EARLY), (EARLY, batch - EARLY)]
+    halves = [(i * (batch // 2), batch // 2) for i in range(2)]
+
+    def to(j, src, dst, sems, k):
+        return pltpu.make_async_remote_copy(
+            src, dst, sems[0].at[k, j - 1], sems[1].at[k, j - 1], device_id={"tp": peer(j)}, device_id_type=MESH
+        )
+
+    def term1(k, j):
+        at = pl.ds(*parts[k])
+        return to(j, t1.at[j - 1, at], rs1.at[j - 1, at], (send1, recv1), k)
+
+    def state1(k, j):
+        at = pl.ds(*parts[k])
+        return to(j, hbuf.at[me, at], hbuf.at[me, at], (gsend1, grecv1), k)
+
+    def term2(k, j):
+        at = pl.ds(*halves[k])
+        return to(j, t2.at[j - 1, at], rs2.at[j - 1, at], (send2, recv2), k)
+
+    def state2(k, j):
+        at = pl.ds(*halves[k])
+        return to(j, ybuf.at[me, at], ybuf.at[me, at], (gsend2, grecv2), k)
+
+    def terms_out(k):
+        at = pl.ds(*parts[k])
         a = seen[at, :].astype(BF16)
-        sent = []
+        for group in by_two:
+            found = [dot(a, wov[:, block_of(j)]) for j in group]
+            for j, t in zip(group, found):
+                if j:
+                    t1[j - 1, at, :] = t.astype(BF16)
+                else:
+                    acc[at, :] = t
+            for j in group:
+                if j:
+                    term1(k, j).start()
+
+    def states_out(k):
+        at = pl.ds(*parts[k])
         for j in order:
-            t1[j - 1, at, :] = dot(a, wov[:, block_of(j)]).astype(BF16)
-            c = pltpu.make_async_remote_copy(
-                t1.at[j - 1, at], rs1.at[j - 1, at], send1.at[part, j - 1], recv1.at[part, j - 1],
-                device_id={"tp": peer(j)}, device_id_type=MESH,
-            )
-            c.start()
-            sent.append(c)
-        acc[at, :] = dot(a, wov[:, block_of(0)])
-        return sent
-
-    def states_out(part, r, many, arrived):
-        at = pl.ds(r, many)
-        for c in arrived:
-            c.wait_recv()
+            term1(k, j).wait_recv()
         total = acc[at, :]
         for j in range(1, n):
             total = total + rs1[j - 1, at, :].astype(F32)
         hbuf[me, at, :] = (xv[at, block_of(0)].astype(F32) + total).astype(BF16)
-        sent = []
         for j in order:
-            c = pltpu.make_async_remote_copy(
-                hbuf.at[me, at], hbuf.at[me, at], gsend1.at[part, j - 1], grecv1.at[part, j - 1],
-                device_id={"tp": peer(j)}, device_id_type=MESH,
-            )
-            c.start()
-            sent.append(c)
-        return sent
-
-    def attend_all(lo, hi):
-        def body(p, carry):
-            attend(p, False)
-            return carry
-
-        lax.fori_loop(lo, hi, body, 0)
-
-    k_in(0).wait()
-    scores(0)
-    k_in(RING).start()
+            state1(k, j).start()
+
+    def states_in(k):
+        for j in order:
+            state1(k, j).wait_recv()
+        r, many = parts[k]
+        for i in range(r, r + many, 16):
+            norm_rows([lambda r, many, s=s: hbuf[s, pl.ds(r, many), :] for s in range(n)], gmf, i, 16)
+
     early_steps = EARLY // PAIR
-    between = early_steps + (steps - early_steps) // 2
-    attend_all(0, early_steps)
-    wo_in.wait()
-    out_a = terms_out(0, 0, EARLY)
-    attend_all(early_steps, between)
-    all_a = states_out(0, 0, EARLY, out_a)
-    attend_all(between, steps - RING)
+    late = (steps - early_steps) // 4
+    scope = jax.named_scope
+
+    def body(p, carry):
+        @pl.when(p == early_steps)
+        def _():
+            with scope("terms_a"):
+                wo_in.wait()
+                terms_out(0)
+
+        @pl.when(p == early_steps + 2 * late)
+        def _():
+            with scope("states_a"):
+                states_out(0)
+
+        @pl.when(p == early_steps + 3 * late)
+        def _():
+            with scope("norm_a"):
+                gm_in.wait()
+                gmf[...] = widened(gmv)
+                states_in(0)
+
+        attend(p, False)
+
+        @pl.when(p == steps - 1 - RING)
+        def _():
+            for c in range(chunks):
+                gate_in(c).start(priority=1)
+                up_in(c).start(priority=1)
+            for j in places:
+                down_in(j).start(priority=1)
+
+        return carry
+
+    with scope("first_scores"):
+        k_in(0).wait()
+        scores(0)
+        k_in(RING).start()
+    with scope("attend"):
+        lax.fori_loop(0, steps - 1, body, 0)
+    with scope("attend_last"):
+        attend(steps - 1, True)
+    with scope("terms_b"):
+        terms_out(1)
+
+    def hidden_out(c, rows):
+        at = pl.ds(*rows)
+        g = dot(normed[at, :], gv[c])
+        u = dot(normed[at, :], uv[c])
+        hidden[at, pl.ds(c * COLS, COLS)] = (jax.nn.silu(g) * u).astype(BF16)
+
     for c in range(chunks):
-        gate_in(c).start()
-        up_in(c).start()
-    for j in order + [0]:
-        down_in(j).start()
-    attend_all(steps - RING, steps - 1)
-    attend(steps - 1, True)
-    out_b = terms_out(1, EARLY, batch - EARLY)
-    all_b = states_out(1, EARLY, batch - EARLY, out_b)
-    for c in all_a + all_b:
-        c.wait_recv()
-
-    gm_in.wait()
-    for r in range(0, batch, 16):
-        norm_rows([lambda r, many, i=i: hbuf[i, pl.ds(r, many), :] for i in range(n)], gmv, r, 16)
-
-    def hidden_step(c, carry):
-        gate_in(c).wait()
-        up_in(c).wait()
-        g = dot(normed[...], gv[c])
-        u = dot(normed[...], uv[c])
-        hidden[:, pl.ds(pl.multiple_of(c * COLS, COLS), COLS)] = (jax.nn.silu(g) * u).astype(BF16)
-        return carry
-
-    lax.fori_loop(0, chunks, hidden_step, 0)
-    sent2 = []
-    for j in order:
-        down_in(j).wait()
-        t2[j - 1] = dot(hidden[...], dv[j]).astype(BF16)
-        c = pltpu.make_async_remote_copy(
-            t2.at[j - 1], rs2.at[j - 1], send2.at[j - 1], recv2.at[j - 1],
-            device_id={"tp": peer(j)}, device_id_type=MESH,
-        )
-        c.start()
-        sent2.append(c)
-    down_in(0).wait()
-    total = dot(hidden[...], dv[0])
-    acc[...] = total
-    for c in sent2:
-        c.wait_recv()
-    total = acc[...]
-    for j in range(1, n):
-        total = total + rs2[j - 1].astype(F32)
-    ybuf[me] = (hbuf[me].astype(F32) + total).astype(BF16)
-    all_y = []
-    for j in order:
-        c = pltpu.make_async_remote_copy(
-            ybuf.at[me], ybuf.at[me], gsend2.at[j - 1], grecv2.at[j - 1],
-            device_id={"tp": peer(j)}, device_id_type=MESH,
-        )
-        c.start()
-        all_y.append(c)
-    for c in all_y:
-        c.wait_recv()
+        if c == chunks // 2:
+            with scope("states_b"):
+                states_out(1)
+        if c == chunks - 1:
+            with scope("norm_b"):
+                states_in(1)
+        with scope("weights_wait"):
+            gate_in(c).wait()
+            up_in(c).wait()
+        with scope("hidden_a"):
+            hidden_out(c, (0, batch) if c == chunks - 1 else parts[0])
+    with scope("hidden_b"):
+        for c in range(chunks - 1):
+            hidden_out(c, parts[1])
+    for group in by_two:
+        with scope("down_wait"):
+            for j in group:
+                down_in(j).wait()
+        with scope("down"):
+            found = [dot(hidden[...], dv[j]) for j in group]
+            for j, t in zip(group, found):
+                if j:
+                    t2[j - 1] = t.astype(BF16)
+                else:
+                    acc[...] = t
+        for k in range(2):
+            for j in group:
+                if j:
+                    term2(k, j).start()
+    for k in range(2):
+        at = pl.ds(*halves[k])
+        with scope("terms2_wait"):
+            for j in order:
+                term2(k, j).wait_recv()
+        total = acc[at, :]
+        for j in range(1, n):
+            total = total + rs2[j - 1, at, :].astype(F32)
+        ybuf[me, at, :] = (hbuf[me, at, :].astype(F32) + total).astype(BF16)
+        for j in order:
+            state2(k, j).start()
+    with scope("states2_wait"):
+        for k in range(2):
+            for j in order:
+                state2(k, j).wait_recv()
     for i in range(n):
         out[:, pl.ds(i * width, width)] = ybuf[i]
-    for c in out_a + out_b + all_a + all_b + sent2 + all_y:
-        c.wait_send()
+    for k in range(2):
+        for j in order:
+            for c in (term1, state1, term2, state2):
+                c(k, j).wait_send()
 
 
 def turns(place, inner):
@@ -293,13 +352,15 @@
         return pl.pallas_call(
             functools.partial(kernel, n),
             name="layer",
-            out_shape=jax.ShapeDtypeStruct((batch, d), BF16),
+            out_shape=pltpu.VMEM((batch, d), BF16),
             in_specs=[anywhere] * 11,
             out_specs=pl.BlockSpec(memory_space=pltpu.VMEM),
             scratch_shapes=[
                 pltpu.VMEM((batch, d), BF16),
-                pltpu.VMEM((1, d), BF16),
-                pltpu.VMEM((1, d), BF16),
+                pltpu.VMEM((d // 128, 128), BF16),
+                pltpu.VMEM((d // 128, 128), BF16),
+                pltpu.VMEM((1, d), F32),
+                pltpu.VMEM((1, d), F32),
                 pltpu.VMEM((2, inner), F32),
                 pltpu.VMEM((ff // COLS, d, COLS), BF16),
                 pltpu.VMEM((ff // COLS, d, COLS), BF16),
@@ -325,13 +386,12 @@
                 dma((2, ff // COLS)),
                 dma((n,)),
             ]
-            + [dma((2, moved))] * 4
-            + [dma((moved,))] * 4,
+            + [dma((2, moved))] * 8,
             compiler_params=pltpu.CompilerParams(
                 collective_id=0, has_side_effects=True, vmem_limit_bytes=VMEM_BYTES
             ),
         )(
-            x, rows_first(k_cache), rows_first(v_cache), gain_a.reshape(1, d), gain_m.reshape(1, d), turn,
+            x, rows_first(k_cache), rows_first(v_cache), gain_a.reshape(-1, 128), gain_m.reshape(-1, 128), turn,
             wq, wo, w_gate, w_up, w_down,
         )
 

time: 108 us -> 92.5 us (0.86)
  Pallas kernels: 104 us -> 91.7 us
  local copies, waits for them, and re-layouts: 4.36 us -> 0.75 us
    pallas_call x1, Pallas kernels: 104 us -> 91.7 us  [step(): pl.pallas_call(functools.partial(kernel, n), name='layer', out_shape=pltp...]
    reshape x2 -> x0, local copies, waits for them, and re-layouts: 2.59 us -> none  [the longest x1 1.3 us: step(): gain_a.reshape(1, d)]
where the time goes in v2:
time: 92.5 us; the launch traced here: 92.4 us
  Pallas kernels  91.7 us (99%)
    pallas_call x1, Pallas kernels, step(): pl.pallas_call(functools.partial(kernel, n), name='layer', out_shape=pltp...  91.7 us

profile of v2, /device:TPU:112, one launch (start us, length us, event | category | flops | bytes accessed | tf_op | source)
XLA Modules:
  0.0 92.4 jit_solution(2265285570965677337)
XLA Ops:
  0.0 91.7 %layer.1 = bf16[64,3072]{1,0:T(8,128)(2,1)S(1)} custom-call(bf16[64,3072]{1,0:T(8,128)(2,1)} %x_hbm.1, bf16[64,768,1024]{2,1,0:T(8,128)(2,1)} %bitcast.1.k_hbm, bf16[64,768,1024]{2,1,0:T(8,128)(2,1)} %bitcast.3.v_hbm, bf16[24,128]{1,0:T(8,128)(2,1)} %bitcast.8, bf16[24,128]{1,0:T(8,128)(2,1)} %bitcast.9, f32[2,768]{1,0:T(2,128)} %constant.2.clone.turn_hbm, ...), custom_call_target="tpu_custom_call" | custom-call | tf_op jit(solution)/shard_map/layer/pallas_call | solution.py:352
  91.7 0.7 copy.13

commit v3 on v2

--- a/solution.py
+++ b/solution.py
@@ -16,6 +16,7 @@
 RING = 3
 COLS = 512
 EARLY = 48
+LATE = 8
 VMEM_BYTES = 66_400_000
 
 
@@ -27,11 +28,13 @@
     return lax.dot_general(a, b, (((1,), (1,)), ((), ())), preferred_element_type=F32)
 
 
-def kernel(n, x_hbm, k_hbm, v_hbm, ga_hbm, gm_hbm, turn_hbm, wq_hbm, wo_hbm, wg_hbm, wu_hbm, wd_hbm, out,
-           xv, gav, gmv, gaf, gmf, turnv, gv, uv, dv, wov, kbuf, vbuf, q_s, s_s, seen, normed, hbuf, hidden,
-           acc, t1, rs1, t2, rs2, ybuf,
-           sem_in, sem_k, sem_v, sem_w, sem_d, send1, recv1, gsend1, grecv1, send2, recv2, gsend2, grecv2):
+def kernel(n, shared, x_hbm, k_hbm, v_hbm, ga_hbm, gm_hbm, turn_hbm, wq_hbm, wo_hbm, wg_hbm, wu_hbm, wd_hbm, out,
+           xv, gav, gmv, gaf, gmf, turnv, gv, uv, dv, wov, kbuf, vbuf, q_s, s_s, normed, hbuf, hidden,
+           acc, t1, rs1, rs2, ybuf, tb, rb, hlate,
+           sem_in, sem_k, sem_v, sem_w, sem_d, send1, recv1, gsend1, grecv1, send2, recv2, gsend2, grecv2, bsend, brecv, csend, crecv):
     batch, d = xv.shape
+    t2 = t1
+    seen = q_s
     width = d // n
     inner = q_s.shape[1]
     heads = inner // HEAD
@@ -55,7 +58,26 @@
     for c in range(0, inner, COLS):
         size = min(COLS, inner - c)
         wq_ins.append((c, size, copy(wq_hbm.at[:, pl.ds(c, size)], gv.at[c // COLS, :, pl.ds(0, size)], sem_w.at[0, c // COLS])))
-    wo_in = copy(wo_hbm, wov, sem_in.at[4])
+
+    group = lax.axis_index("dp")
+    core = lax.rem(group, 2)
+
+    def half_of(many):
+        return pl.ds(pl.multiple_of(core * (many // 2), many // 2), many // 2) if shared else pl.ds(0, many)
+
+    def handed(ref, k):
+        return pltpu.make_async_remote_copy(
+            ref, ref, csend.at[k], crecv.at[k], device_id={"dp": group + 1 - 2 * core}, device_id_type=MESH
+        )
+
+    ups = 0 if shared else 0
+    wo_in = copy(wo_hbm.at[half_of(inner)], wov.at[half_of(inner)], sem_in.at[4])
+
+    def up_half_in(c):
+        return copy(wu_hbm.at[half_of(d), pl.ds(c * COLS, COLS)], uv.at[c, half_of(d)], sem_w.at[1, c])
+
+    hands = [handed(wov.at[half_of(inner)], ups)] if shared else []
+    up_hands = [handed(uv.at[c, half_of(d)], c) for c in range(ups)]
 
     def k_in(p):
         slot = lax.rem(p, RING)
@@ -84,12 +106,16 @@
         k_in(p).start()
         v_in(p).start()
     wo_in.start()
+    for c in range(ups):
+        up_half_in(c).start()
 
     with jax.named_scope("entry"):
         barrier = pltpu.get_barrier_semaphore()
         for j in range(1, n):
             pl.semaphore_signal(barrier, inc=1, device_id={"tp": peer(j)}, device_id_type=MESH)
-        pl.semaphore_wait(barrier, n - 1)
+        if shared:
+            pl.semaphore_signal(barrier, inc=1, device_id={"dp": group + 1 - 2 * core}, device_id_type=MESH)
+        pl.semaphore_wait(barrier, n if shared else n - 1)
 
     def widened(gain):
         g = gain[...].astype(F32)
@@ -165,7 +191,6 @@
     places = order + [0]
     by_two = [places[i : i + 2] for i in range(0, n, 2)]
     parts = [(0, EARLY), (EARLY, batch - EARLY)]
-    halves = [(i * (batch // 2), batch // 2) for i in range(2)]
 
     def to(j, src, dst, sems, k):
         return pltpu.make_async_remote_copy(
@@ -181,12 +206,40 @@
         return to(j, hbuf.at[me, at], hbuf.at[me, at], (gsend1, grecv1), k)
 
     def term2(k, j):
-        at = pl.ds(*halves[k])
+        at = pl.ds(*parts[k])
         return to(j, t2.at[j - 1, at], rs2.at[j - 1, at], (send2, recv2), k)
 
     def state2(k, j):
-        at = pl.ds(*halves[k])
+        at = pl.ds(*parts[k])
         return to(j, ybuf.at[me, at], ybuf.at[me, at], (gsend2, grecv2), k)
+
+    def late_term(k, j):
+        return to(j, tb.at[k], rb.at[k, me], (bsend, brecv), k)
+
+    late_rows = pl.ds(EARLY, batch - EARLY)
+
+    def late_out(k):
+        t = dot(seen[late_rows, :].astype(BF16), wov[...])[k * LATE : (k + 1) * LATE].astype(BF16)
+        tb[k] = t
+        rb[k, me] = t
+        for j in order:
+            late_term(k, j).start()
+
+    def late_in(k):
+        for j in order:
+            late_term(k, j).wait_recv()
+        total = rb[k, 0].astype(F32)
+        for i in range(1, n):
+            total = total + rb[k, i].astype(F32)
+        at = pl.ds(k * LATE, LATE)
+        h = xv[late_rows, :].astype(F32)[k * LATE : (k + 1) * LATE] + total
+        hlate[at, :] = h.astype(BF16).astype(F32)
+
+    def late_norm():
+        wide = hlate[...]
+        scale = lax.rsqrt(jnp.mean(wide * wide, -1, keepdims=True) + 1e-6)
+        normed[late_rows, :] = (wide * scale * gmf[...]).astype(BF16)
+        hbuf[me, late_rows, :] = hlate[:, block_of(0)].astype(BF16)
 
     def terms_out(k):
         at = pl.ds(*parts[k])
@@ -220,38 +273,49 @@
         for i in range(r, r + many, 16):
             norm_rows([lambda r, many, s=s: hbuf[s, pl.ds(r, many), :] for s in range(n)], gmf, i, 16)
 
+    units = [u for c in range(chunks) for u in ((gate_in(c),) if c < ups else (gate_in(c), up_in(c)))] + [down_in(j) for j in places]
+    started = [0]
+
+    def start(many):
+        for u in units[started[0] : started[0] + many]:
+            u.start(priority=1)
+        started[0] += many
+
     early_steps = EARLY // PAIR
-    late = (steps - early_steps) // 4
     scope = jax.named_scope
 
     def body(p, carry):
+        if shared:
+            @pl.when(p == early_steps // 4)
+            def _():
+                with scope("hand"):
+                    wo_in.wait()
+                    for c in range(ups):
+                        up_half_in(c).wait()
+                    for h in hands + up_hands:
+                        h.start()
+
         @pl.when(p == early_steps)
         def _():
             with scope("terms_a"):
-                wo_in.wait()
+                if not shared:
+                    wo_in.wait()
+                for h in hands:
+                    h.wait_recv()
                 terms_out(0)
 
-        @pl.when(p == early_steps + 2 * late)
+        @pl.when(p == steps - LATE // PAIR)
         def _():
             with scope("states_a"):
                 states_out(0)
-
-        @pl.when(p == early_steps + 3 * late)
-        def _():
-            with scope("norm_a"):
-                gm_in.wait()
-                gmf[...] = widened(gmv)
-                states_in(0)
+            with scope("terms_m"):
+                late_out(0)
 
         attend(p, False)
 
         @pl.when(p == steps - 1 - RING)
         def _():
-            for c in range(chunks):
-                gate_in(c).start(priority=1)
-                up_in(c).start(priority=1)
-            for j in places:
-                down_in(j).start(priority=1)
+            start(4)
 
         return carry
 
@@ -262,48 +326,73 @@
     with scope("attend"):
         lax.fori_loop(0, steps - 1, body, 0)
     with scope("attend_last"):
+        start(2)
         attend(steps - 1, True)
+        start(2)
     with scope("terms_b"):
-        terms_out(1)
-
-    def hidden_out(c, rows):
+        late_out(1)
+        start(2)
+
+    def hidden_out(cs, rows):
         at = pl.ds(*rows)
-        g = dot(normed[at, :], gv[c])
-        u = dot(normed[at, :], uv[c])
-        hidden[at, pl.ds(c * COLS, COLS)] = (jax.nn.silu(g) * u).astype(BF16)
-
-    for c in range(chunks):
-        if c == chunks // 2:
-            with scope("states_b"):
-                states_out(1)
-        if c == chunks - 1:
-            with scope("norm_b"):
-                states_in(1)
-        with scope("weights_wait"):
+        for c in cs:
+            g = dot(normed[at, :], gv[c])
+            u = dot(normed[at, :], uv[c])
+            hidden[at, pl.ds(c * COLS, COLS)] = (jax.nn.silu(g) * u).astype(BF16)
+
+    def weights_in(cs):
+        for c in cs:
             gate_in(c).wait()
-            up_in(c).wait()
-        with scope("hidden_a"):
-            hidden_out(c, (0, batch) if c == chunks - 1 else parts[0])
+            if c < ups:
+                up_hands[c].wait_recv()
+            else:
+                up_in(c).wait()
+
+    former, latter = range(chunks // 2), range(chunks // 2, chunks)
+    with scope("norm_a"):
+        gm_in.wait()
+        gmf[...] = widened(gmv)
+        states_in(0)
+        for j in order:
+            term1(0, j).wait_send()
+        late_in(0)
+    with scope("weights_wait"):
+        weights_in(former)
+    with scope("hidden_a"):
+        hidden_out(former, parts[0])
+        start(n - 2)
+    with scope("norm_b"):
+        late_in(1)
+        late_norm()
+    with scope("weights_wait"):
+        weights_in(latter)
+    with scope("hidden_ab"):
+        hidden_out(latter, (0, batch))
+
+    def down_out(k):
+        at = pl.ds(*parts[k])
+        for group in by_two:
+            if k == 0:
+                with scope("down_wait"):
+                    for j in group:
+                        down_in(j).wait()
+            with scope("down"):
+                found = [dot(hidden[at, :], dv[j]) for j in group]
+                for j, t in zip(group, found):
+                    if j:
+                        t2[j - 1, at, :] = t.astype(BF16)
+                    else:
+                        acc[at, :] = t
+                for j in group:
+                    if j:
+                        term2(k, j).start()
+
+    down_out(0)
     with scope("hidden_b"):
-        for c in range(chunks - 1):
-            hidden_out(c, parts[1])
-    for group in by_two:
-        with scope("down_wait"):
-            for j in group:
-                down_in(j).wait()
-        with scope("down"):
-            found = [dot(hidden[...], dv[j]) for j in group]
-            for j, t in zip(group, found):
-                if j:
-                    t2[j - 1] = t.astype(BF16)
-                else:
-                    acc[...] = t
-        for k in range(2):
-            for j in group:
-                if j:
-                    term2(k, j).start()
+        hidden_out(former, parts[1])
+    down_out(1)
     for k in range(2):
-        at = pl.ds(*halves[k])
+        at = pl.ds(*parts[k])
         with scope("terms2_wait"):
             for j in order:
                 term2(k, j).wait_recv()
@@ -315,14 +404,19 @@
             state2(k, j).start()
     with scope("states2_wait"):
         for k in range(2):
+            at = pl.ds(*parts[k])
             for j in order:
                 state2(k, j).wait_recv()
-    for i in range(n):
-        out[:, pl.ds(i * width, width)] = ybuf[i]
+            for i in range(n):
+                out[at, pl.ds(i * width, width)] = ybuf[i, at, :]
+    for h in hands + up_hands:
+        h.wait_send()
     for k in range(2):
         for j in order:
-            for c in (term1, state1, term2, state2):
+            for c in (late_term, term2, state2):
                 c(k, j).wait_send()
+            if k == 0:
+                state1(k, j).wait_send()
 
 
 def turns(place, inner):
@@ -335,6 +429,7 @@
 
 def solution(mesh):
     n = mesh.shape["tp"]
+    shared = 2 if mesh.shape["dp"] % 2 == 0 else 0
 
     def step(x, k_cache, v_cache, gain_a, wq, wo, gain_m, w_gate, w_up, w_down):
         batch, d = x.shape
@@ -350,7 +445,7 @@
         dma = pltpu.SemaphoreType.DMA
         moved = n - 1
         return pl.pallas_call(
-            functools.partial(kernel, n),
+            functools.partial(kernel, n, shared),
             name="layer",
             out_shape=pltpu.VMEM((batch, d), BF16),
             in_specs=[anywhere] * 11,
@@ -370,23 +465,25 @@
                 pltpu.VMEM((RING, PAIR, inner, places), BF16),
                 pltpu.VMEM((batch, inner), F32),
                 pltpu.VMEM((PAIR * heads, places), F32),
-                pltpu.VMEM((batch, inner), F32),
                 pltpu.VMEM((batch, d), BF16),
                 pltpu.VMEM((n, batch, width), BF16),
                 pltpu.VMEM((batch, ff), BF16),
                 pltpu.VMEM((batch, width), F32),
                 pltpu.VMEM((moved, batch, width), BF16),
-                pltpu.VMEM((moved, batch, width), BF16),
-                pltpu.VMEM((moved, batch, width), BF16),
+                pltpu.VMEM((moved, EARLY, width), BF16),
                 pltpu.VMEM((moved, batch, width), BF16),
                 pltpu.VMEM((n, batch, width), BF16),
+                pltpu.VMEM((2, LATE, d), BF16),
+                pltpu.VMEM((2, n, LATE, d), BF16),
+                pltpu.VMEM((2 * LATE, d), F32),
                 dma((5,)),
                 dma((RING,)),
                 dma((RING,)),
                 dma((2, ff // COLS)),
                 dma((n,)),
             ]
-            + [dma((2, moved))] * 8,
+            + [dma((2, moved))] * 10
+            + [dma((3,))] * 2,
             compiler_params=pltpu.CompilerParams(
                 collective_id=0, has_side_effects=True, vmem_limit_bytes=VMEM_BYTES
             ),

time: 92.5 us -> 88.3 us (0.955)
  Pallas kernels: 91.7 us -> 87.5 us
    pallas_call x1, Pallas kernels: 91.7 us -> 87.5 us  [step(): pl.pallas_call(functools.partial(kernel, n, shared), name='layer', out_sh...]
where the time goes in v3:
time: 88.3 us; the launch traced here: 88.2 us
  Pallas kernels  87.5 us (99%)
    pallas_call x1, Pallas kernels, step(): pl.pallas_call(functools.partial(kernel, n, shared), name='layer', out_sh...  87.5 us

profile of v3, /device:TPU:112, one launch (start us, length us, event | category | flops | bytes accessed | tf_op | source)
XLA Modules:
  0.0 88.2 jit_solution(10068374814843939298)
XLA Ops:
  0.0 87.5 %layer.1 = bf16[64,3072]{1,0:T(8,128)(2,1)S(1)} custom-call(bf16[64,3072]{1,0:T(8,128)(2,1)} %x_hbm.1, bf16[64,768,1024]{2,1,0:T(8,128)(2,1)} %bitcast.1.k_hbm, bf16[64,768,1024]{2,1,0:T(8,128)(2,1)} %bitcast.3.v_hbm, bf16[24,128]{1,0:T(8,128)(2,1)} %bitcast.8, bf16[24,128]{1,0:T(8,128)(2,1)} %bitcast.9, f32[2,768]{1,0:T(2,128)} %constant.2.clone.turn_hbm, ...), custom_call_target="tpu_custom_call" | custom-call | tf_op jit(solution)/shard_map/layer/pallas_call | solution.py:447
  87.5 0.7 copy.13

commit v4 on v3

--- a/solution.py
+++ b/solution.py
@@ -54,10 +54,6 @@
     ga_in = copy(ga_hbm, gav, sem_in.at[1])
     gm_in = copy(gm_hbm, gmv, sem_in.at[2])
     turn_in = copy(turn_hbm, turnv, sem_in.at[3])
-    wq_ins = []
-    for c in range(0, inner, COLS):
-        size = min(COLS, inner - c)
-        wq_ins.append((c, size, copy(wq_hbm.at[:, pl.ds(c, size)], gv.at[c // COLS, :, pl.ds(0, size)], sem_w.at[0, c // COLS])))
 
     group = lax.axis_index("dp")
     core = lax.rem(group, 2)
@@ -72,6 +68,14 @@
 
     ups = 0 if shared else 0
     wo_in = copy(wo_hbm.at[half_of(inner)], wov.at[half_of(inner)], sem_in.at[4])
+
+    wq_ins, wq_hands = [], []
+    for i, c in enumerate(range(0, inner, COLS)):
+        size = min(COLS, inner - c)
+        to_ref = gv.at[i, half_of(d), pl.ds(0, size)]
+        wq_ins.append((c, size, copy(wq_hbm.at[half_of(d), pl.ds(c, size)], to_ref, sem_w.at[0, i])))
+        if shared:
+            wq_hands.append(handed(to_ref, 1 + i))
 
     def up_half_in(c):
         return copy(wu_hbm.at[half_of(d), pl.ds(c * COLS, COLS)], uv.at[c, half_of(d)], sem_w.at[1, c])
@@ -103,9 +107,9 @@
         c.start()
     gm_in.start()
     for p in range(RING):
-        k_in(p).start()
-        v_in(p).start()
-    wo_in.start()
+        k_in(p).start(priority=1)
+        v_in(p).start(priority=1)
+    wo_in.start(priority=1)
     for c in range(ups):
         up_half_in(c).start()
 
@@ -130,6 +134,9 @@
             at = pl.ds(i * step, step)
             normed[pl.ds(r, many), at] = (w * scale * gain[:, at]).astype(BF16)
 
+    for h, (_, _, c_in) in zip(wq_hands, wq_ins):
+        c_in.wait()
+        h.start()
     with jax.named_scope("x_wait"):
         x_in.wait()
         ga_in.wait()
@@ -137,9 +144,12 @@
     for r in range(0, batch, 16):
         norm_rows([lambda r, many: xv[pl.ds(r, many), :]], gaf, r, 16)
     turn_in.wait()
-    for c, size, c_in in wq_ins:
+    for i, (c, size, c_in) in enumerate(wq_ins):
         with jax.named_scope("wq_wait"):
-            c_in.wait()
+            if shared:
+                wq_hands[i].wait_recv()
+            else:
+                c_in.wait()
         q_s[:, pl.ds(c, size)] = dot(normed[...], gv[c // COLS, :, pl.ds(0, size)])
     half = HEAD // 2
     lane = lax.broadcasted_iota(jnp.int32, (16, inner), 1)
@@ -289,6 +299,8 @@
             @pl.when(p == early_steps // 4)
             def _():
                 with scope("hand"):
+                    for h in wq_hands:
+                        h.wait_send()
                     wo_in.wait()
                     for c in range(ups):
                         up_half_in(c).wait()

time: 88.3 us -> 88.7 us (level)
  no operation moved by 1% of the time
where the time goes in v4:
time: 88.7 us; the launch traced here: 88.4 us
  Pallas kernels  87.6 us (99%)
    pallas_call x1, Pallas kernels, step(): pl.pallas_call(functools.partial(kernel, n, shared), name='layer', out_sh...  87.6 us

profile of v4, /device:TPU:112, one launch (start us, length us, event | category | flops | bytes accessed | tf_op | source)
XLA Modules:
  0.0 88.4 jit_solution(3152567490840983222)
XLA Ops:
  0.0 87.6 %layer.1 = bf16[64,3072]{1,0:T(8,128)(2,1)S(1)} custom-call(bf16[64,3072]{1,0:T(8,128)(2,1)} %x_hbm.1, bf16[64,768,1024]{2,1,0:T(8,128)(2,1)} %bitcast.1.k_hbm, bf16[64,768,1024]{2,1,0:T(8,128)(2,1)} %bitcast.3.v_hbm, bf16[24,128]{1,0:T(8,128)(2,1)} %bitcast.8, bf16[24,128]{1,0:T(8,128)(2,1)} %bitcast.9, f32[2,768]{1,0:T(2,128)} %constant.2.clone.turn_hbm, ...), custom_call_target="tpu_custom_call" | custom-call | tf_op jit(solution)/shard_map/layer/pallas_call | solution.py:459
  87.6 0.7 copy.13
